TPU v7x, 32 devices: a whole 2x2x4 slice. The times are simulated.
32 devices in a mesh: group: 2 (over y), dev: 16 (over z, x, core).
Axes of the slice: x: 2, y: 2, z: 4, core: 2. Of those that a mesh axis runs over, the one named last changes fastest.
Arguments:
- bin_index: int32 [131072, 128], P(('group', 'dev')), may hold values from 0 to 63
- gradient: bfloat16 [131072], P(('group', 'dev')), may hold values from -6 to 6
- hessian: bfloat16 [131072], P(('group', 'dev')), may hold values from 0.049804688 to 0.25
- child_id: int32 [131072], P(('group', 'dev')), may hold values from 0 to 63
- smaller_side: int32 [32], replicated, may hold values from 0 to 1
Outputs:
- best_gain: float32 [32, 128], P('group', 'dev')
- child_best: float32 [32], P('group')
All inputs are finite; a program needn't handle non-finite values.
Results may differ from a plain program's by a relative error of at most 0.0003.
Values sent between devices are 32-bit elements; how exact they have to be, the bound alone decides.
A program may use at most 64 MiB of HBM per device.

v0:
```python
import functools

import jax
import jax.numpy as jnp
from jax import lax
from jax.experimental import pallas as pl
from jax.experimental.pallas import tpu as pltpu
from jax.sharding import PartitionSpec as P

BINS = 64
LANES = 128
KCHUNK = 1024
STEP_ROWS = 512


reg_lambda = 1.0


def split_gains(hist_grad, hist_hess):
    left_grad = jnp.cumsum(hist_grad, axis=-1)[..., :-1]
    left_hess = jnp.cumsum(hist_hess, axis=-1)[..., :-1]
    total_grad = jnp.sum(hist_grad, axis=-1, keepdims=True)
    total_hess = jnp.sum(hist_hess, axis=-1, keepdims=True)
    right_grad = total_grad - left_grad
    value = left_grad * left_grad / (left_hess + reg_lambda)
    value = value + right_grad * right_grad / (total_hess - left_hess + reg_lambda)
    value = value - total_grad * total_grad / (total_hess + reg_lambda)
    return jnp.max(value, axis=-1)


def plain_body(bin_index, gradient, hessian, child_id, smaller_side):
    leaves = smaller_side.shape[0]
    features = bin_index.shape[1]
    target = 2 * jnp.arange(leaves, dtype=jnp.int32)[None, :] + smaller_side[None, :]
    chosen = child_id[:, None] == target
    nothing = jnp.zeros((), jnp.bfloat16)
    weights = jnp.concatenate(
        [
            jnp.where(chosen, gradient[:, None], nothing),
            jnp.where(chosen, hessian[:, None], nothing),
        ],
        axis=1,
    )
    levels = jnp.arange(BINS, dtype=jnp.int32)

    def one_feature(column):
        onehot = (column[:, None] == levels[None, :]).astype(jnp.bfloat16)
        product = lax.dot_general(
            weights, onehot, (((0,), (0,)), ((), ())), preferred_element_type=jnp.float32
        )
        return product.reshape(2, leaves, BINS).transpose(1, 0, 2).reshape(leaves, 2 * BINS)

    stacked = lax.map(one_feature, bin_index.T)
    owned = lax.psum_scatter(stacked, "dev", scatter_dimension=0, tiled=True)
    owned = lax.psum_scatter(owned, "group", scatter_dimension=1, tiled=True)
    hist_grad = owned[:, :, :BINS].transpose(1, 0, 2)
    hist_hess = owned[:, :, BINS:].transpose(1, 0, 2)
    best_gain = split_gains(hist_grad, hist_hess)
    child_best = lax.pmax(jnp.max(best_gain, axis=1), "dev")
    return (best_gain, child_best)


def kernel(
    groups, devs, leaves,
    bins_ref, grad_ref, hess_ref, child_ref, side_ref,
    gain_ref, best_ref,
    bins_v, grad_v, hess_v, child_v, values, bins_sem, small_sem,
    bins_t, weights, pair_out, pair_in, side_out, side_in, mine, far_in, near_in, best_out, best_in,
    pair_send, pair_recv, side_send, side_recv, far_send, far_recv, near_send, near_recv,
    best_send, best_recv,
):
    rows, features = bins_ref.shape
    own_features = features // devs
    own_leaves = leaves // groups
    width = 2 * own_leaves
    slots = LANES // width
    quads = own_features // slots
    chips = devs // 2
    me_g = lax.axis_index("group")
    me_d = lax.axis_index("dev")
    me_c = lax.rem(me_d, 2)
    me_j = lax.div(me_d, 2)
    planes = chips // 2
    me_x = lax.rem(me_j, 2)
    me_z = lax.div(me_j, 2)
    barrier = pltpu.get_barrier_semaphore()
    step_rows = STEP_ROWS

    def bins_copy(number):
        here = pl.ds(pl.multiple_of(number * step_rows, step_rows), step_rows)
        return pltpu.make_async_copy(bins_ref.at[here, :], bins_v.at[here, :], bins_sem.at[number])

    small = [
        pltpu.make_async_copy(source, place, small_sem.at[number])
        for number, (source, place) in enumerate(
            [(grad_ref, grad_v), (hess_ref, hess_v), (child_ref, child_v)]
        )
    ]
    for copy in small:
        copy.start()

    def at(g, d):
        return {"group": g, "dev": d}

    greeted = 0
    for step in range(1, devs):
        other = lax.rem(me_d + step, devs)
        pl.semaphore_signal(barrier, inc=1, device_id=at(me_g, other), device_id_type=pl.DeviceIdType.MESH)
        greeted += 1
    for turn in range(1, groups):
        for step in range(chips):
            other = lax.rem(me_j + step, chips) * 2 + me_c
            pl.semaphore_signal(
                barrier, inc=1, device_id=at(lax.rem(me_g + turn, groups), other),
                device_id_type=pl.DeviceIdType.MESH,
            )
            greeted += 1

    columns = groups * LANES
    column = lax.broadcasted_iota(jnp.int32, (columns, 1), 0)
    within = lax.rem(column, width)
    leaf = lax.div(column, LANES) * own_leaves + lax.rem(within, own_leaves)
    target = jnp.zeros_like(leaf)
    for number in range(leaves):
        target = jnp.where(leaf == number, 2 * number + side_ref[number], target)
    is_grad = within < own_leaves

    lax.fori_loop(0, rows // step_rows, lambda number, carry: (bins_copy(number).start(), carry)[1], 0)
    for copy in small:
        copy.wait()
    values[0] = grad_v[...].astype(jnp.float32)
    values[1] = hess_v[...].astype(jnp.float32)

    def prepare(number, carry):
        bins_copy(number).wait()
        here = pl.ds(pl.multiple_of(number * step_rows, step_rows), step_rows)
        bins_t[:, here] = bins_v[here, :].astype(jnp.float32).T
        for piece in range(step_rows // LANES):
            row = number * (step_rows // LANES) + piece
            value = jnp.where(is_grad, values[0, pl.ds(row, 1), :], values[1, pl.ds(row, 1), :])
            value = jnp.where(child_v[pl.ds(row, 1), :] == target, value, 0.0)
            there = pl.ds(pl.multiple_of(row * LANES, LANES), LANES)
            weights[there, :] = value.T.astype(jnp.bfloat16)
        return carry

    lax.fori_loop(0, rows // step_rows, prepare, 0)

    chunk = min(rows, KCHUNK)
    pack = 16
    level = lax.broadcasted_iota(jnp.int32, (pack, chunk), 0).astype(jnp.float32).astype(jnp.bfloat16)
    one = jnp.ones((), jnp.bfloat16)
    zero = jnp.zeros((), jnp.bfloat16)
    lane = lax.broadcasted_iota(jnp.int32, (BINS, LANES), 1)

    def block(d):
        base = pl.multiple_of(d * own_features, own_features)
        total = None
        for start in range(0, rows, chunk):
            parts = []
            levels = bins_t[pl.ds(base, own_features), start:start + chunk]
            for f in range(own_features):
                row = jnp.broadcast_to(levels[f:f + 1, :], (pack, chunk)).astype(jnp.bfloat16)
                for low in range(0, BINS, pack):
                    parts.append(jnp.where(row == level + jnp.bfloat16(low), one, zero))
            onehot = jnp.concatenate(parts, axis=0)
            product = jnp.dot(onehot, weights[start:start + chunk, :], preferred_element_type=jnp.float32)
            total = product if total is None else total + product
        result = []
        for g in range(groups):
            for q in range(quads):
                piece = None
                for s in range(slots):
                    f = q * slots + s
                    here = total[f * BINS:(f + 1) * BINS, g * LANES:(g + 1) * LANES]
                    piece = here if piece is None else jnp.where(lane >= s * width, here, piece)
                result.append(piece)
        return result

    def pair_copy(j):
        return pltpu.make_async_remote_copy(
            src_ref=pair_out.at[j], dst_ref=pair_in.at[j],
            send_sem=pair_send.at[j], recv_sem=pair_recv.at[j],
            device_id=at(me_g, me_j * 2 + 1 - me_c), device_id_type=pl.DeviceIdType.MESH,
        )

    def side_copy(k):
        return pltpu.make_async_remote_copy(
            src_ref=side_out.at[k], dst_ref=side_in.at[k],
            send_sem=side_send.at[k], recv_sem=side_recv.at[k],
            device_id=at(me_g, (me_z * 2 + 1 - me_x) * 2 + me_c), device_id_type=pl.DeviceIdType.MESH,
        )

    def far_copy(k, turn):
        to_g = lax.rem(me_g + turn, groups)
        return pltpu.make_async_remote_copy(
            src_ref=mine.at[k, to_g], dst_ref=far_in.at[turn, k],
            send_sem=far_send.at[turn, k], recv_sem=far_recv.at[turn, k],
            device_id=at(to_g, (lax.rem(me_z + 1 + k, planes) * 2 + me_x) * 2 + me_c),
            device_id_type=pl.DeviceIdType.MESH,
        )

    def near_copy(turn):
        to_g = lax.rem(me_g + turn, groups)
        return pltpu.make_async_remote_copy(
            src_ref=side_out.at[planes - 1, to_g], dst_ref=near_in.at[turn],
            send_sem=near_send.at[turn], recv_sem=near_recv.at[turn],
            device_id=at(to_g, (me_z * 2 + 1 - me_x) * 2 + me_c), device_id_type=pl.DeviceIdType.MESH,
        )

    def owner(j):
        to_z = lax.rem(me_z + 1 + lax.div(j, 2), planes)
        to_x = lax.rem(me_x + 1 + lax.rem(j, 2), 2)
        return (to_z * 2 + to_x) * 2

    def send_pair(j, first=False):
        pieces = block(owner(j) + 1 - me_c)
        if first:
            pl.semaphore_wait(barrier, greeted)
        for g in range(groups):
            for q in range(quads):
                pair_out[j, g, q * BINS:(q + 1) * BINS, :] = pieces[g * quads + q]
        pair_copy(j).start()

    send_pair(0, True)

    def one_step(j, carry):
        k = lax.div(j, 2)
        odd = lax.rem(j, 2)

        @pl.when(j < chips - 1)
        def _():
            send_pair(j + 1)

        pieces = block(owner(j) + me_c)
        pair_copy(j).wait()

        def put(ref):
            for g in range(groups):
                for q in range(quads):
                    part = slice(q * BINS, (q + 1) * BINS)
                    ref[k, g, part, :] = pieces[g * quads + q] + pair_in[j, g, part, :]

        @pl.when(odd == 0)
        def _():
            put(side_out)

            @pl.when(k < planes - 1)
            def _():
                side_copy(k).start()

            @pl.when(k == planes - 1)
            def _():
                for turn in range(groups):
                    near_copy(turn).start()

            @pl.when(k > 0)
            def _():
                side_copy(k - 1).wait()
                for g in range(groups):
                    mine[k - 1, g] = mine[k - 1, g] + side_in[k - 1, g]
                for turn in range(groups):
                    far_copy(k - 1, turn).start()

        @pl.when(odd == 1)
        def _():
            put(mine)

            @pl.when(k == planes - 1)
            def _():
                for turn in range(1, groups):
                    far_copy(planes - 1, turn).start()

        return carry

    lax.fori_loop(0, chips, one_step, 0)

    hist = mine[planes - 1, me_g]
    for k in range(planes - 1):
        for turn in range(groups):
            far_copy(k, turn).wait()
            hist = hist + far_in[turn, k]
    for turn in range(groups):
        near_copy(turn).wait()
        hist = hist + near_in[turn]
    for turn in range(1, groups):
        far_copy(planes - 1, turn).wait()
        hist = hist + far_in[turn, planes - 1]

    bests = []
    for q in range(quads):
        left = hist[q * BINS:(q + 1) * BINS, :]
        shift = 1
        while shift < BINS:
            left = left + jnp.concatenate(
                [jnp.zeros((shift, LANES), jnp.float32), left[:BINS - shift, :]], axis=0
            )
            shift *= 2
        both = pltpu.roll(left, LANES - own_leaves, 1)
        left_grad, left_hess = left, both
        total_grad, total_hess = left[BINS - 1:, :], both[BINS - 1:, :]
        right_grad = total_grad - left_grad
        usable = lax.rem(lane, width) < own_leaves
        left_hess = jnp.where(usable, left_hess, 0.0)
        total_hess = jnp.where(usable[:1, :], total_hess, 0.0)
        value = left_grad * left_grad / (left_hess + reg_lambda)
        value = value + right_grad * right_grad / (total_hess - left_hess + reg_lambda)
        value = value - total_grad * total_grad / (total_hess + reg_lambda)
        row = lax.broadcasted_iota(jnp.int32, (BINS, LANES), 0)
        value = jnp.where(row < BINS - 1, value, -jnp.inf)
        bests.append(jnp.max(value, axis=0, keepdims=True))
    best = bests[0]
    for q in range(quads):
        gain_ref[q:q + 1, :] = bests[q]
        best = jnp.maximum(best, bests[q])
    best = jnp.broadcast_to(best, (8, LANES))
    move = width
    folded = best
    for s in range(1, slots):
        folded = jnp.maximum(folded, pltpu.roll(best, s * move, 1))
    best_out[...] = folded

    def best_copy(step):
        return pltpu.make_async_remote_copy(
            src_ref=best_out, dst_ref=best_in.at[step],
            send_sem=best_send.at[step], recv_sem=best_recv.at[step],
            device_id=at(me_g, lax.rem(me_d + step, devs)), device_id_type=pl.DeviceIdType.MESH,
        )

    for step in range(1, devs):
        best_copy(step).start()
    for step in range(1, devs):
        best_copy(step).wait()
        folded = jnp.maximum(folded, best_in[step])
    best_ref[...] = folded


def kernel_body(groups, devs, bin_index, gradient, hessian, child_id, smaller_side):
    rows, features = bin_index.shape
    leaves = smaller_side.shape[0]
    own_features = features // devs
    own_leaves = leaves // groups
    width = 2 * own_leaves
    slots = LANES // width
    quads = own_features // slots
    chips = devs // 2
    planes = chips // 2
    vmem = pl.BlockSpec(memory_space=pltpu.VMEM)
    hbm = pl.BlockSpec(memory_space=pltpu.HBM)
    gain, best = pl.pallas_call(
        functools.partial(kernel, groups, devs, leaves),
        out_shape=(
            jax.ShapeDtypeStruct((quads, LANES), jnp.float32),
            jax.ShapeDtypeStruct((8, LANES), jnp.float32),
        ),
        in_specs=[hbm, hbm, hbm, hbm, pl.BlockSpec(memory_space=pltpu.SMEM)],
        out_specs=(vmem, vmem),
        scratch_shapes=[
            pltpu.VMEM((rows, features), jnp.int32),
            pltpu.VMEM((rows // LANES, LANES), jnp.bfloat16),
            pltpu.VMEM((rows // LANES, LANES), jnp.bfloat16),
            pltpu.VMEM((rows // LANES, LANES), jnp.int32),
            pltpu.VMEM((2, rows // LANES, LANES), jnp.float32),
            pltpu.SemaphoreType.DMA((rows // STEP_ROWS,)),
            pltpu.SemaphoreType.DMA((3,)),
            pltpu.VMEM((features, rows), jnp.float32),
            pltpu.VMEM((rows, groups * LANES), jnp.bfloat16),
            pltpu.VMEM((chips, groups, quads * BINS, LANES), jnp.float32),
            pltpu.VMEM((chips, groups, quads * BINS, LANES), jnp.float32),
            pltpu.VMEM((planes, groups, quads * BINS, LANES), jnp.float32),
            pltpu.VMEM((planes, groups, quads * BINS, LANES), jnp.float32),
            pltpu.VMEM((planes, groups, quads * BINS, LANES), jnp.float32),
            pltpu.VMEM((groups, planes, quads * BINS, LANES), jnp.float32),
            pltpu.VMEM((groups, quads * BINS, LANES), jnp.float32),
            pltpu.VMEM((8, LANES), jnp.float32),
            pltpu.VMEM((devs, 8, LANES), jnp.float32),
            pltpu.SemaphoreType.DMA((chips,)),
            pltpu.SemaphoreType.DMA((chips,)),
            pltpu.SemaphoreType.DMA((planes,)),
            pltpu.SemaphoreType.DMA((planes,)),
            pltpu.SemaphoreType.DMA((groups, planes)),
            pltpu.SemaphoreType.DMA((groups, planes)),
            pltpu.SemaphoreType.DMA((groups,)),
            pltpu.SemaphoreType.DMA((groups,)),
            pltpu.SemaphoreType.DMA((devs,)),
            pltpu.SemaphoreType.DMA((devs,)),
        ],
        compiler_params=pltpu.CompilerParams(
            collective_id=0, has_side_effects=True, vmem_limit_bytes=63 * 1024 * 1024
        ),
    )(
        bin_index, gradient.reshape(rows // LANES, LANES), hessian.reshape(rows // LANES, LANES),
        child_id.reshape(rows // LANES, LANES), smaller_side,
    )
    best_gain = gain.reshape(quads, slots, width)[:, :, :own_leaves]
    best_gain = best_gain.transpose(2, 0, 1).reshape(own_leaves, own_features)
    return (best_gain, best[0, :own_leaves])


def fits(groups, devs, leaves, features, rows):
    if devs % 4 or devs < 8 or features % devs or leaves % groups:
        return False
    width = 2 * (leaves // groups)
    if LANES % width:
        return False
    slots = LANES // width
    own = features // devs
    return own % slots == 0 and own % 8 == 0 and rows % KCHUNK == 0 and devs <= 16


def solution(mesh):
    in_specs = (
        P(("group", "dev"), None),
        P(("group", "dev")),
        P(("group", "dev")),
        P(("group", "dev")),
        P(),
    )
    out_specs = (P("group", "dev"), P("group"))
    groups, devs = mesh.shape["group"], mesh.shape["dev"]

    def body(bin_index, gradient, hessian, child_id, smaller_side):
        rows, features = bin_index.shape
        args = (bin_index, gradient, hessian, child_id, smaller_side)
        if fits(groups, devs, smaller_side.shape[0], features, rows):
            return kernel_body(groups, devs, *args)
        return plain_body(*args)

    return jax.shard_map(body, mesh=mesh, in_specs=in_specs, out_specs=out_specs, check_vma=False)
```

profile of v0, /device:TPU:0, one launch (start us, length us, event | category | flops | bytes accessed | tf_op | source)
XLA Modules:
  0.0 42.7 jit_solution(1280069303370376417)
XLA Ops:
  0.6 39.5 %shard_map.68 = (f32[2,128]{1,0:T(2,128)}, f32[8,128]{1,0:T(8,128)}) custom-call(s32[4096,128]{1,0:T(8,128)} %bins_ref.1, bf16[32,128]{1,0:T(8,128)(2,1)} %bitcast.10, bf16[32,128]{1,0:T(8,128)(2,1)} %bitcast.11, s32[32,128]{1,0:T(8,128)} %bitcast.9, s32[32]{0:T(128)} %side_ref.1), custom_call_target="tpu_custom_call" | custom-call | tf_op jit(solution)/shard_map/pallas_call | solution.py:349
  40.2 1.2 %slice_bitcast_fusion = f32[16]{0:T(128)} fusion(f32[8,128]{1,0:T(8,128)} %get-tuple-element.5), kind=kLoop, calls=%fused_computation | loop fusion | bytes 128 | tf_op jit(solution)/shard_map/squeeze | solution.py:396
  41.4 1.3 %reshape.22 = f32[2,4,32]{2,1,0:T(4,128)} reshape(f32[2,128]{1,0:T(2,128)} %get-tuple-element.4) | data formatting | bytes 2048 | tf_op jit(solution)/shard_map/reshape | solution.py:394
where the time goes:
time: 43 us; the launch traced here: 42.7 us
  Pallas kernels  39.5 us (92%)
  local copies, waits for them, and re-layouts  2.51 us (6%)
  between operations  0.64 us (1%)
    pallas_call x1, Pallas kernels, kernel_body(): pl.pallas_call(functools.partial(kernel, groups, devs, leaves), out_shape...  39.5 us
    reshape x1, local copies, waits for them, and re-layouts, kernel_body(): best_gain = gain.reshape(quads, slots, width)[:, :, :own_leaves]  1.33 us
    squeeze x1, local copies, waits for them, and re-layouts, kernel_body(): return (best_gain, best[0, :own_leaves])  1.18 us

commit v1 on v0

v1 whole, which is shorter than its diff:
```python
import functools

import jax
import jax.numpy as jnp
from jax import lax
from jax.experimental import pallas as pl
from jax.experimental.pallas import tpu as pltpu
from jax.sharding import PartitionSpec as P

BINS = 64
LANES = 128
KCHUNK = 1024
STEP_ROWS = 512


reg_lambda = 1.0


def split_gains(hist_grad, hist_hess):
    left_grad = jnp.cumsum(hist_grad, axis=-1)[..., :-1]
    left_hess = jnp.cumsum(hist_hess, axis=-1)[..., :-1]
    total_grad = jnp.sum(hist_grad, axis=-1, keepdims=True)
    total_hess = jnp.sum(hist_hess, axis=-1, keepdims=True)
    right_grad = total_grad - left_grad
    value = left_grad * left_grad / (left_hess + reg_lambda)
    value = value + right_grad * right_grad / (total_hess - left_hess + reg_lambda)
    value = value - total_grad * total_grad / (total_hess + reg_lambda)
    return jnp.max(value, axis=-1)


def plain_body(bin_index, gradient, hessian, child_id, smaller_side):
    leaves = smaller_side.shape[0]
    features = bin_index.shape[1]
    target = 2 * jnp.arange(leaves, dtype=jnp.int32)[None, :] + smaller_side[None, :]
    chosen = child_id[:, None] == target
    nothing = jnp.zeros((), jnp.bfloat16)
    weights = jnp.concatenate(
        [
            jnp.where(chosen, gradient[:, None], nothing),
            jnp.where(chosen, hessian[:, None], nothing),
        ],
        axis=1,
    )
    levels = jnp.arange(BINS, dtype=jnp.int32)

    def one_feature(column):
        onehot = (column[:, None] == levels[None, :]).astype(jnp.bfloat16)
        product = lax.dot_general(
            weights, onehot, (((0,), (0,)), ((), ())), preferred_element_type=jnp.float32
        )
        return product.reshape(2, leaves, BINS).transpose(1, 0, 2).reshape(leaves, 2 * BINS)

    stacked = lax.map(one_feature, bin_index.T)
    owned = lax.psum_scatter(stacked, "dev", scatter_dimension=0, tiled=True)
    owned = lax.psum_scatter(owned, "group", scatter_dimension=1, tiled=True)
    hist_grad = owned[:, :, :BINS].transpose(1, 0, 2)
    hist_hess = owned[:, :, BINS:].transpose(1, 0, 2)
    best_gain = split_gains(hist_grad, hist_hess)
    child_best = lax.pmax(jnp.max(best_gain, axis=1), "dev")
    return (best_gain, child_best)


def kernel(
    groups, devs, leaves,
    bins_ref, grad_ref, hess_ref, child_ref, side_ref,
    done_ref,
    bins_v, side_v, grad_v, hess_v, child_v, values, bins_sem, small_sem,
    bins_t, weights, out, pair_in, a_in, b_in, c_in, d_in, e_in, f_out, f_in, near_in,
    gain_out, gain_in, best_in,
    pair_sem, a_sem, b_sem, c_sem, d_sem, e_sem, f_sem, near_sem, gain_sem, best_sem,
):
    rows, features = bins_ref.shape
    per_dev = features // devs
    own_features = per_dev // groups
    own_leaves = leaves // groups
    width = 2 * leaves
    slots = LANES // width
    quads = own_features // slots
    half = quads // 2
    planes = devs // 4
    last = planes - 1
    relayed = last - 1
    me_g = lax.axis_index("group")
    me_d = lax.axis_index("dev")
    me_c = lax.rem(me_d, 2)
    me_j = lax.div(me_d, 2)
    me_x = lax.rem(me_j, 2)
    me_z = lax.div(me_j, 2)
    barrier = pltpu.get_barrier_semaphore()
    step_rows = STEP_ROWS
    everyone = groups * devs

    def bins_copy(number):
        here = pl.ds(pl.multiple_of(number * step_rows, step_rows), step_rows)
        return pltpu.make_async_copy(bins_ref.at[here, :], bins_v.at[here, :], bins_sem.at[number])

    small = [
        pltpu.make_async_copy(source, place, small_sem.at[number])
        for number, (source, place) in enumerate(
            [(side_ref, side_v), (child_ref, child_v), (grad_ref, grad_v), (hess_ref, hess_v)]
        )
    ]
    for copy in small:
        copy.start()

    def start_bins(number, carry):
        bins_copy(number).start()
        return carry

    lax.fori_loop(0, rows // step_rows, start_bins, 0)

    def at(g, d):
        return {"group": g, "dev": d}

    def nth(step):
        other = lax.rem(me_g * devs + me_d + step, everyone)
        return at(lax.div(other, devs), lax.rem(other, devs))

    def greet(step, carry):
        pl.semaphore_signal(barrier, inc=1, device_id=nth(step), device_id_type=pl.DeviceIdType.MESH)
        return carry

    lax.fori_loop(1, everyone, greet, 0)

    pair_row = lax.broadcasted_iota(jnp.int32, (leaves, leaves), 0)
    pair_lane = lax.broadcasted_iota(jnp.int32, (leaves, leaves), 1)

    for copy in small:
        copy.wait()

    side = jnp.where(pair_lane == pair_row, side_v[...].astype(jnp.float32), 0.0)
    target = jnp.sum(side, axis=1, keepdims=True) + 2.0 * pair_row[:, :1].astype(jnp.float32)
    target = jnp.broadcast_to(target, (leaves, LANES)).astype(jnp.bfloat16)
    values[0] = grad_v[...].astype(jnp.float32)
    values[1] = hess_v[...].astype(jnp.float32)
    values[2] = child_v[...].astype(jnp.float32)
    no_weight = jnp.zeros((), jnp.bfloat16)

    def prepare(number, carry):
        here = pl.ds(pl.multiple_of(number * step_rows, step_rows), step_rows)
        for piece in range(step_rows // LANES):
            row = number * (step_rows // LANES) + piece
            there = pl.ds(pl.multiple_of(row * LANES, LANES), LANES)

            def spread(kind):
                return jnp.broadcast_to(values[kind, pl.ds(row, 1), :], (leaves, LANES)).astype(jnp.bfloat16)

            chosen = spread(2) == target
            for kind in range(2):
                value = jnp.where(chosen, spread(kind), no_weight)
                for s in range(slots):
                    start = s * width + kind * leaves
                    weights[start:start + leaves, there] = value
        bins_copy(number).wait()
        bins_t[:, here] = bins_v[here, :].astype(jnp.float32).T
        return carry

    lax.fori_loop(0, rows // step_rows, prepare, 0)

    chunk = min(rows, KCHUNK)
    pack = 16
    level = lax.broadcasted_iota(jnp.int32, (pack, chunk), 0).astype(jnp.float32).astype(jnp.bfloat16)
    one = jnp.ones((), jnp.bfloat16)
    zero = jnp.zeros((), jnp.bfloat16)
    lane = lax.broadcasted_iota(jnp.int32, (BINS, LANES), 1)

    def block(d):
        base = pl.multiple_of(d * per_dev, per_dev)
        total = None
        for start in range(0, rows, chunk):
            parts = []
            levels = bins_t[pl.ds(base, per_dev), start:start + chunk]
            for f in range(per_dev):
                row = jnp.broadcast_to(levels[f:f + 1, :], (pack, chunk)).astype(jnp.bfloat16)
                for low in range(0, BINS, pack):
                    parts.append(jnp.where(row <= level + jnp.bfloat16(low), one, zero))
            below = jnp.concatenate(parts, axis=0)
            product = lax.dot_general(
                below, weights[:, start:start + chunk], (((1,), (1,)), ((), ())),
                preferred_element_type=jnp.float32,
            )
            total = product if total is None else total + product
        result = []
        for y in range(groups):
            for q in range(quads):
                piece = None
                for s in range(slots):
                    f = (y * quads + q) * slots + s
                    here = total[f * BINS:(f + 1) * BINS, :]
                    piece = here if piece is None else jnp.where(lane >= s * width, here, piece)
                result.append((y, q, piece))
        return result

    def remote(source, place, sem, index, device):
        return pltpu.make_async_remote_copy(
            src_ref=source, dst_ref=place, send_sem=sem.at[0, index], recv_sem=sem.at[1, index],
            device_id=device, device_id_type=pl.DeviceIdType.MESH,
        )

    def pick(index, choices):
        result = choices[-1]
        for number in range(len(choices) - 1):
            result = jnp.where(index == number, choices[number], result)
        return result

    def flipped(turn):
        result, bit = 0, 1
        while bit < planes:
            digit = lax.rem(lax.div(me_z, bit), 2)
            result = result + bit * (1 - digit if (turn // bit) % 2 else digit)
            bit *= 2
        return result

    planes_of = [flipped(last - k) for k in range(planes)]

    def plane(k):
        return planes_of[k] if isinstance(k, int) else pick(k, planes_of)

    def dev_of(k, dx, core):
        x = jnp.where(dx == 1, 1 - me_x, me_x)
        return (plane(k) * 2 + x) * 2 + core

    pair_dev = at(me_g, me_j * 2 + 1 - me_c)
    x_dev_d = (me_z * 2 + 1 - me_x) * 2 + me_c
    x_dev = at(me_g, x_dev_d)
    y_g = 1 - me_g
    y_dev = at(y_g, me_d)
    diag_dev = at(y_g, x_dev_d)

    def pair_copy(n):
        return remote(out.at[0, n], pair_in.at[n], pair_sem, n, pair_dev)

    first = slice(0, half)
    second = slice(half, quads)

    def a_copy(k):
        return remote(out.at[1, 2 * k + 1, first], a_in.at[k], a_sem, k, x_dev)

    def b_copy(k):
        return remote(out.at[1, 2 * k + 1, second, me_g], b_in.at[k], b_sem, k, x_dev)

    def c_copy(k):
        return remote(out.at[1, 2 * k + 1, second, y_g], c_in.at[k], c_sem, k, y_dev)

    def d_copy(k):
        return remote(out.at[1, 2 * k, second, y_g], d_in.at[k], d_sem, k, y_dev)

    def e_copy(k):
        return remote(out.at[1, 2 * k, first, y_g], e_in.at[k], e_sem, k, y_dev)

    def f_copy(k):
        d = (plane(k) * 2 + me_x) * 2 + me_c
        return remote(f_out.at[k], f_in.at[k], f_sem, k, at(me_g, d))

    def direct_copy(k, n):
        dx, y = ((1, y_g), (1, me_g), (0, y_g), (0, me_g))[n]
        d = dev_of(k, dx, me_c)
        return remote(out.at[1, 2 * k + dx, :, y], near_in.at[k - relayed, n], near_sem, (k - relayed) * 4 + n, at(y, d))

    def direct(k):
        return range(3 if k == last else 4)

    def do_b(k):
        c_copy(k).wait_recv()
        out[1, 2 * k + 1, second, me_g] = out[1, 2 * k + 1, second, me_g] + c_in[k]
        b_copy(k).start()

    def do_e(k):
        a_copy(k).wait_recv()
        out[1, 2 * k, first, y_g] = out[1, 2 * k, first, y_g] + a_in[k, :, y_g]
        e_copy(k).start()

    def do_f(k):
        b_copy(k).wait_recv()
        d_copy(k).wait_recv()
        f_out[k, second] = out[1, 2 * k, second, me_g] + b_in[k] + d_in[k]
        e_copy(k).wait_recv()
        f_out[k, first] = out[1, 2 * k, first, me_g] + a_in[k, :, me_g] + e_in[k]
        f_copy(k).start()

    steps = [(k, dx) for dx in (1, 0) for k in range(relayed)]
    steps += [(last, 1), (relayed, 1), (relayed, 0), (last, 0)]
    total_steps = len(steps)

    def iteration(turn, carry):
        is_p = jnp.logical_or(turn == 0, jnp.logical_and(lax.rem(turn, 2) == 1, turn < 2 * total_steps - 1))
        step = jnp.where(is_p, lax.div(turn + 1, 2), lax.div(jnp.maximum(turn - 1, 0), 2))
        k = pick(step, [a for a, _ in steps])
        dx = pick(step, [a for _, a in steps])
        n = 2 * k + dx
        role = jnp.where(is_p, 0, 1)
        for y, q, piece in block(dev_of(k, dx, jnp.where(is_p, 1 - me_c, me_c))):
            out[role, n, q, y] = piece

        @pl.when(turn == 0)
        def _():
            pl.semaphore_wait(barrier, everyone - 1)

        @pl.when(is_p)
        def _():
            pair_copy(n).start()

            @pl.when(step >= relayed + 3)
            def _():
                @pl.when(step < 2 * relayed + 3)
                def _():
                    do_f(step - relayed - 3)

        @pl.when(jnp.logical_not(is_p))
        def _():
            pair_copy(n).wait_recv()
            out[1, n] = out[1, n] + pair_in[n]

            @pl.when(k < relayed)
            def _():
                @pl.when(dx == 1)
                def _():
                    a_copy(k).start()
                    c_copy(k).start()

                @pl.when(dx == 0)
                def _():
                    d_copy(k).start()
                    do_e(k)
                    do_b(k)

            @pl.when(k >= relayed)
            def _():
                @pl.when(dx == 1)
                def _():
                    direct_copy(k, 0).start()
                    direct_copy(k, 1).start()

                @pl.when(dx == 0)
                def _():
                    direct_copy(k, 2).start()

                    @pl.when(k < last)
                    def _():
                        direct_copy(k, 3).start()

        return carry

    lax.fori_loop(0, 2 * total_steps, iteration, 0)

    hist = out[1, 2 * last, :, me_g]
    for k in range(relayed):
        f_copy(k).wait_recv()
        hist = hist + f_in[k]
    for k in range(relayed, planes):
        for number in direct(k):
            direct_copy(k, number).wait_recv()
            hist = hist + near_in[k - relayed, number]

    usable = lax.rem(lane, width) < leaves
    keep = lax.broadcasted_iota(jnp.int32, (BINS, LANES), 0) < BINS - 1
    lane8 = lax.broadcasted_iota(jnp.int32, (8, LANES), 1)
    row8 = lax.broadcasted_iota(jnp.int32, (8, LANES), 0)
    tile = jnp.full((8, LANES), -jnp.inf, jnp.float32)
    for q in range(quads):
        left_grad = hist[q]
        left_hess = jnp.where(usable, pltpu.roll(left_grad, LANES - leaves, 1), 0.0)
        total_grad, total_hess = left_grad[BINS - 1:, :], left_hess[BINS - 1:, :]
        right_grad = total_grad - left_grad
        value = left_grad * left_grad / (left_hess + reg_lambda)
        value = value + right_grad * right_grad / (total_hess - left_hess + reg_lambda)
        value = value - total_grad * total_grad / (total_hess + reg_lambda)
        value = jnp.where(keep, value, -jnp.inf)
        best = jnp.broadcast_to(jnp.max(value, axis=0, keepdims=True), (8, LANES))
        for s in range(slots):
            moved = pltpu.roll(best, LANES - s * width, 1) if s else best
            tile = jnp.where(row8 == q * slots + s, moved, tile)
    top = jnp.max(tile, axis=0, keepdims=True)
    tile = jnp.where(row8 == 7, top, tile)
    gain_out[...] = tile

    gain_copy = remote(gain_out, gain_in, gain_sem, 0, y_dev)
    gain_copy.start()

    def best_copy(step):
        return remote(gain_out.at[pl.ds(7, 1)], best_in.at[step], best_sem, step, nth(step))

    for step in range(1, everyone):
        if step != devs:
            best_copy(step).start()
    for n in range(2 * planes):
        pair_copy(n).wait_send()
    for k in range(relayed):
        for make in (a_copy, b_copy, c_copy, d_copy, e_copy, f_copy):
            make(k).wait_send()
    for k in range(relayed, planes):
        for number in direct(k):
            direct_copy(k, number).wait_send()
    gain_copy.wait()
    other = gain_in[...]
    top = jnp.maximum(top, other[7:8, :])
    low_tile = jnp.where(me_g == 0, tile, other)
    high_tile = jnp.where(me_g == 0, other, tile)
    gain = jnp.where(row8 < own_features, low_tile, pltpu.roll(high_tile, own_features, 0))
    done_ref[0] = jnp.where(me_g == 0, gain, pltpu.roll(gain, LANES - own_leaves, 1))
    for step in range(1, everyone):
        if step != devs:
            best_copy(step).wait()
            top = jnp.maximum(top, best_in[step])
    top = jnp.broadcast_to(top, (8, LANES))
    done_ref[1] = jnp.where(me_g == 0, top, pltpu.roll(top, LANES - own_leaves, 1))


def finish(done_ref, gain_ref, best_ref):
    gain_ref[...] = done_ref[0, :gain_ref.shape[0], :gain_ref.shape[1]]
    best_ref[...] = done_ref[1, 0, :best_ref.shape[0]]


def kernel_body(groups, devs, bin_index, gradient, hessian, child_id, smaller_side):
    rows, features = bin_index.shape
    leaves = smaller_side.shape[0]
    per_dev = features // devs
    own_features = per_dev // groups
    own_leaves = leaves // groups
    slots = LANES // (2 * leaves)
    quads = own_features // slots
    half = quads // 2
    planes = devs // 4
    relayed = planes - 2
    everyone = groups * devs
    vmem = pl.BlockSpec(memory_space=pltpu.VMEM)
    hbm = pl.BlockSpec(memory_space=pltpu.HBM)

    def floats(*shape):
        return pltpu.VMEM(shape + (BINS, LANES), jnp.float32)

    def sems(number):
        return pltpu.SemaphoreType.DMA((2, number))

    done = pl.pallas_call(
        functools.partial(kernel, groups, devs, leaves),
        out_shape=jax.ShapeDtypeStruct((2, 8, LANES), jnp.float32),
        in_specs=[hbm] * 5,
        out_specs=vmem,
        scratch_shapes=[
            pltpu.VMEM((rows, features), jnp.int32),
            pltpu.VMEM((1, leaves), jnp.int32),
            pltpu.VMEM((rows // LANES, LANES), jnp.bfloat16),
            pltpu.VMEM((rows // LANES, LANES), jnp.bfloat16),
            pltpu.VMEM((rows // LANES, LANES), jnp.int32),
            pltpu.VMEM((3, rows // LANES, LANES), jnp.float32),
            pltpu.SemaphoreType.DMA((rows // STEP_ROWS,)),
            pltpu.SemaphoreType.DMA((4,)),
            pltpu.VMEM((features, rows), jnp.float32),
            pltpu.VMEM((LANES, rows), jnp.bfloat16),
            floats(2, 2 * planes, quads, groups),
            floats(2 * planes, quads, groups),
            floats(relayed, half, groups),
            floats(relayed, half),
            floats(relayed, half),
            floats(relayed, half),
            floats(relayed, half),
            floats(relayed, quads),
            floats(relayed, quads),
            floats(2, 4, quads),
            pltpu.VMEM((8, LANES), jnp.float32),
            pltpu.VMEM((8, LANES), jnp.float32),
            pltpu.VMEM((everyone, 1, LANES), jnp.float32),
            sems(2 * planes),
            sems(relayed),
            sems(relayed),
            sems(relayed),
            sems(relayed),
            sems(relayed),
            sems(relayed),
            sems(8),
            sems(1),
            sems(everyone),
        ],
        compiler_params=pltpu.CompilerParams(
            collective_id=0, has_side_effects=True, vmem_limit_bytes=63 * 1024 * 1024
        ),
    )(
        bin_index, gradient.reshape(rows // LANES, LANES), hessian.reshape(rows // LANES, LANES),
        child_id.reshape(rows // LANES, LANES), smaller_side.reshape(1, leaves),
    )
    gain, best = pl.pallas_call(
        finish,
        out_shape=(
            jax.ShapeDtypeStruct((per_dev, own_leaves), jnp.float32),
            jax.ShapeDtypeStruct((own_leaves,), jnp.float32),
        ),
        in_specs=[vmem],
        out_specs=(vmem, vmem),
    )(done)
    return (gain.T, best)


def fits(groups, devs, leaves, features, rows):
    planes = devs // 4
    if groups != 2 or devs % 4 or planes != 4 or leaves != 32:
        return False
    return features == 8 * devs and rows % KCHUNK == 0


def solution(mesh):
    in_specs = (
        P(("group", "dev"), None),
        P(("group", "dev")),
        P(("group", "dev")),
        P(("group", "dev")),
        P(),
    )
    out_specs = (P("group", "dev"), P("group"))
    groups, devs = mesh.shape["group"], mesh.shape["dev"]

    def body(bin_index, gradient, hessian, child_id, smaller_side):
        rows, features = bin_index.shape
        args = (bin_index, gradient, hessian, child_id, smaller_side)
        if fits(groups, devs, smaller_side.shape[0], features, rows):
            return kernel_body(groups, devs, *args)
        return plain_body(*args)

    return jax.shard_map(body, mesh=mesh, in_specs=in_specs, out_specs=out_specs, check_vma=False)
```

time: 43 us -> 39.6 us (0.921)
  local copies, waits for them, and re-layouts: 2.51 us -> 0 us
  Pallas kernels: 39.5 us -> 38.8 us
    pallas_call x1, Pallas kernels: 39.5 us -> 37.5 us  [kernel_body(): pl.pallas_call(functools.partial(kernel, groups, devs, leaves), out_shape...]
    reshape x1 -> x0, local copies, waits for them, and re-layouts: 1.33 us -> none  [kernel_body(): best_gain = gain.reshape(quads, slots, width)[:, :, :own_leaves]]
    pallas_call x0 -> x1, Pallas kernels: none -> 1.29 us  [kernel_body(): pl.pallas_call(finish, out_shape=(jax.ShapeDtypeStruct((per_dev, own_leav...]
    squeeze x1 -> x0, local copies, waits for them, and re-layouts: 1.18 us -> none  [kernel_body(): return (best_gain, best[0, :own_leaves])]
where the time goes in v1:
time: 39.6 us; the launch traced here: 39.4 us
  Pallas kernels  38.8 us (98%)
  between operations  0.64 us (2%)
    pallas_call x1, Pallas kernels, kernel_body(): pl.pallas_call(functools.partial(kernel, groups, devs, leaves), out_shape...  37.5 us
    pallas_call x1, Pallas kernels, kernel_body(): pl.pallas_call(finish, out_shape=(jax.ShapeDtypeStruct((per_dev, own_leav...  1.29 us

profile of v1, /device:TPU:0, one launch (start us, length us, event | category | flops | bytes accessed | tf_op | source)
XLA Modules:
  0.0 39.4 jit_solution(9428917230490926377)
XLA Ops:
  0.6 37.5 %shard_map.68.done_ref = f32[2,8,128]{2,1,0:T(8,128)} custom-call(s32[4096,128]{1,0:T(8,128)} %bins_ref.1, bf16[32,128]{1,0:T(8,128)(2,1)} %bitcast.6, bf16[32,128]{1,0:T(8,128)(2,1)} %bitcast.7, s32[32,128]{1,0:T(8,128)} %bitcast.5, s32[1,32]{1,0:T(1,128)} %bitcast.8), custom_call_target="tpu_custom_call" | custom-call | tf_op jit(solution)/shard_map/pallas_call | solution.py:435
  38.1 1.3 %shard_map.69 = (f32[8,16]{1,0:T(8,128)}, f32[16]{0:T(128)}) custom-call(f32[2,8,128]{2,1,0:T(8,128)} %shard_map.68.done_ref), custom_call_target="tpu_custom_call" | custom-call | tf_op jit(solution)/shard_map/pallas_call | solution.py:482

commit v2 on v1

--- a/solution.py
+++ b/solution.py
@@ -10,7 +10,7 @@
 BINS = 64
 LANES = 128
 KCHUNK = 1024
-STEP_ROWS = 512
+STEP_ROWS = 1024
 
 
 reg_lambda = 1.0
@@ -279,69 +279,84 @@
         f_copy(k).start()
 
     steps = [(k, dx) for dx in (1, 0) for k in range(relayed)]
-    steps += [(last, 1), (relayed, 1), (relayed, 0), (last, 0)]
+    steps += [(relayed, 1), (last, 1), (relayed, 0), (last, 0)]
     total_steps = len(steps)
 
-    def iteration(turn, carry):
-        is_p = jnp.logical_or(turn == 0, jnp.logical_and(lax.rem(turn, 2) == 1, turn < 2 * total_steps - 1))
-        step = jnp.where(is_p, lax.div(turn + 1, 2), lax.div(jnp.maximum(turn - 1, 0), 2))
+    def group_of(step):
         k = pick(step, [a for a, _ in steps])
         dx = pick(step, [a for _, a in steps])
-        n = 2 * k + dx
+        return k, dx, 2 * k + dx
+
+    def work(step, is_p):
+        k, dx, n = group_of(step)
         role = jnp.where(is_p, 0, 1)
         for y, q, piece in block(dev_of(k, dx, jnp.where(is_p, 1 - me_c, me_c))):
             out[role, n, q, y] = piece
 
+    def send_pair(step):
+        pair_copy(group_of(step)[2]).start()
+
+    def pass_on(step, carry):
+        k, dx, n = group_of(step)
+        pair_copy(n).wait_recv()
+        out[1, n] = out[1, n] + pair_in[n]
+
+        @pl.when(k < relayed)
+        def _():
+            @pl.when(dx == 1)
+            def _():
+                a_copy(k).start()
+                c_copy(k).start()
+
+            @pl.when(dx == 0)
+            def _():
+                d_copy(k).start()
+                do_e(k)
+                do_b(k)
+
+        @pl.when(k >= relayed)
+        def _():
+            @pl.when(dx == 1)
+            def _():
+                direct_copy(k, 0).start()
+                direct_copy(k, 1).start()
+
+            @pl.when(dx == 0)
+            def _():
+                direct_copy(k, 2).start()
+
+                @pl.when(k < last)
+                def _():
+                    direct_copy(k, 3).start()
+
+        return carry
+
+    def iteration(turn, carry):
+        work(jnp.maximum(turn - 1, 0), turn == 0)
+        work(jnp.minimum(turn + 1, total_steps - 1), turn < total_steps - 1)
+
         @pl.when(turn == 0)
         def _():
             pl.semaphore_wait(barrier, everyone - 1)
-
-        @pl.when(is_p)
+            send_pair(0)
+
+        @pl.when(turn < total_steps - 1)
         def _():
-            pair_copy(n).start()
-
-            @pl.when(step >= relayed + 3)
+            send_pair(turn + 1)
+
+        lax.fori_loop(
+            jnp.maximum(turn - 1, 0), jnp.where(turn == total_steps - 1, total_steps, turn), pass_on, 0
+        )
+
+        @pl.when(turn >= 2 * relayed + 1)
+        def _():
+            @pl.when(turn < 2 * relayed + 1 + relayed)
             def _():
-                @pl.when(step < 2 * relayed + 3)
-                def _():
-                    do_f(step - relayed - 3)
-
-        @pl.when(jnp.logical_not(is_p))
-        def _():
-            pair_copy(n).wait_recv()
-            out[1, n] = out[1, n] + pair_in[n]
-
-            @pl.when(k < relayed)
-            def _():
-                @pl.when(dx == 1)
-                def _():
-                    a_copy(k).start()
-                    c_copy(k).start()
-
-                @pl.when(dx == 0)
-                def _():
-                    d_copy(k).start()
-                    do_e(k)
-                    do_b(k)
-
-            @pl.when(k >= relayed)
-            def _():
-                @pl.when(dx == 1)
-                def _():
-                    direct_copy(k, 0).start()
-                    direct_copy(k, 1).start()
-
-                @pl.when(dx == 0)
-                def _():
-                    direct_copy(k, 2).start()
-
-                    @pl.when(k < last)
-                    def _():
-                        direct_copy(k, 3).start()
+                do_f(turn - (2 * relayed + 1))
 
         return carry
 
-    lax.fori_loop(0, 2 * total_steps, iteration, 0)
+    lax.fori_loop(0, total_steps, iteration, 0)
 
     hist = out[1, 2 * last, :, me_g]
     for k in range(relayed):

time: 39.6 us -> 39 us (0.985)
  Pallas kernels: 38.8 us -> 38.2 us
    pallas_call x1, Pallas kernels: 37.5 us -> 36.9 us  [kernel_body(): pl.pallas_call(functools.partial(kernel, groups, devs, leaves), out_shape...]
where the time goes in v2:
time: 39 us; the launch traced here: 38.8 us
  Pallas kernels  38.2 us (98%)
  between operations  0.64 us (2%)
    pallas_call x1, Pallas kernels, kernel_body(): pl.pallas_call(functools.partial(kernel, groups, devs, leaves), out_shape...  36.9 us
    pallas_call x1, Pallas kernels, kernel_body(): pl.pallas_call(finish, out_shape=(jax.ShapeDtypeStruct((per_dev, own_leav...  1.29 us

profile of v2, /device:TPU:0, one launch (start us, length us, event | category | flops | bytes accessed | tf_op | source)
XLA Modules:
  0.0 38.8 jit_solution(8296310617667866300)
XLA Ops:
  0.6 36.9 %shard_map.68.done_ref = f32[2,8,128]{2,1,0:T(8,128)} custom-call(s32[4096,128]{1,0:T(8,128)} %bins_ref.1, bf16[32,128]{1,0:T(8,128)(2,1)} %bitcast.6, bf16[32,128]{1,0:T(8,128)(2,1)} %bitcast.7, s32[32,128]{1,0:T(8,128)} %bitcast.5, s32[1,32]{1,0:T(1,128)} %bitcast.8), custom_call_target="tpu_custom_call" | custom-call | tf_op jit(solution)/shard_map/pallas_call | solution.py:450
  37.5 1.3 %shard_map.69 = (f32[8,16]{1,0:T(8,128)}, f32[16]{0:T(128)}) custom-call(f32[2,8,128]{2,1,0:T(8,128)} %shard_map.68.done_ref), custom_call_target="tpu_custom_call" | custom-call | tf_op jit(solution)/shard_map/pallas_call | solution.py:497

commit v3 on v2

--- a/solution.py
+++ b/solution.py
@@ -151,11 +151,16 @@
                 for s in range(slots):
                     start = s * width + kind * leaves
                     weights[start:start + leaves, there] = value
+        return carry
+
+    def turn_bins(number, carry):
+        here = pl.ds(pl.multiple_of(number * step_rows, step_rows), step_rows)
         bins_copy(number).wait()
-        bins_t[:, here] = bins_v[here, :].astype(jnp.float32).T
+        bins_t[:, here] = bins_v[here, :].astype(jnp.float32).astype(jnp.bfloat16).T.astype(jnp.float32)
         return carry
 
     lax.fori_loop(0, rows // step_rows, prepare, 0)
+    lax.fori_loop(0, rows // step_rows, turn_bins, 0)
 
     chunk = min(rows, KCHUNK)
     pack = 16
@@ -278,9 +283,8 @@
         f_out[k, first] = out[1, 2 * k, first, me_g] + a_in[k, :, me_g] + e_in[k]
         f_copy(k).start()
 
-    steps = [(k, dx) for dx in (1, 0) for k in range(relayed)]
-    steps += [(relayed, 1), (last, 1), (relayed, 0), (last, 0)]
-    total_steps = len(steps)
+    steps = [(k, 1) for k in range(last)] + [(k, 0) for k in range(last)] + [(last, 1), (last, 0)]
+    turns = len(steps)
 
     def group_of(step):
         k = pick(step, [a for a, _ in steps])
@@ -293,10 +297,7 @@
         for y, q, piece in block(dev_of(k, dx, jnp.where(is_p, 1 - me_c, me_c))):
             out[role, n, q, y] = piece
 
-    def send_pair(step):
-        pair_copy(group_of(step)[2]).start()
-
-    def pass_on(step, carry):
+    def pass_on(step):
         k, dx, n = group_of(step)
         pair_copy(n).wait_recv()
         out[1, n] = out[1, n] + pair_in[n]
@@ -329,34 +330,47 @@
                 def _():
                     direct_copy(k, 3).start()
 
-        return carry
-
     def iteration(turn, carry):
-        work(jnp.maximum(turn - 1, 0), turn == 0)
-        work(jnp.minimum(turn + 1, total_steps - 1), turn < total_steps - 1)
+        step = lax.div(turn, 2) * 2
+        is_p = lax.rem(turn, 2) == 0
+        work(step, is_p)
+        work(step + 1, is_p)
 
         @pl.when(turn == 0)
         def _():
             pl.semaphore_wait(barrier, everyone - 1)
-            send_pair(0)
-
-        @pl.when(turn < total_steps - 1)
+
+        @pl.when(is_p)
         def _():
-            send_pair(turn + 1)
-
-        lax.fori_loop(
-            jnp.maximum(turn - 1, 0), jnp.where(turn == total_steps - 1, total_steps, turn), pass_on, 0
-        )
-
-        @pl.when(turn >= 2 * relayed + 1)
+            pair_copy(group_of(step)[2]).start()
+            pair_copy(group_of(step + 1)[2]).start()
+
+        @pl.when(jnp.logical_not(is_p))
         def _():
-            @pl.when(turn < 2 * relayed + 1 + relayed)
-            def _():
-                do_f(turn - (2 * relayed + 1))
+            for k in range(relayed - 1):
+                @pl.when(turn == turns - 1 - 2 * (relayed - 1 - k))
+                def _():
+                    do_f(k)
+
+            pass_on(step)
+            pass_on(step + 1)
 
         return carry
 
-    lax.fori_loop(0, total_steps, iteration, 0)
+    lax.fori_loop(0, turns - 1, iteration, 0)
+
+    def closing(step, carry):
+        work(step, False)
+
+        pass_on(step)
+
+        @pl.when(step == turns - 2)
+        def _():
+            do_f(relayed - 1)
+
+        return carry
+
+    lax.fori_loop(turns - 2, turns, closing, 0)
 
     hist = out[1, 2 * last, :, me_g]
     for k in range(relayed):

time: 39 us -> 37.7 us (0.967)
  Pallas kernels: 38.2 us -> 36.8 us
    pallas_call x1, Pallas kernels: 36.9 us -> 35.5 us  [kernel_body(): pl.pallas_call(functools.partial(kernel, groups, devs, leaves), out_shape...]
where the time goes in v3:
time: 37.7 us; the launch traced here: 37.5 us
  Pallas kernels  36.8 us (98%)
  between operations  0.64 us (2%)
    pallas_call x1, Pallas kernels, kernel_body(): pl.pallas_call(functools.partial(kernel, groups, devs, leaves), out_shape...  35.5 us
    pallas_call x1, Pallas kernels, kernel_body(): pl.pallas_call(finish, out_shape=(jax.ShapeDtypeStruct((per_dev, own_leav...  1.29 us

profile of v3, /device:TPU:0, one launch (start us, length us, event | category | flops | bytes accessed | tf_op | source)
XLA Modules:
  0.0 37.5 jit_solution(7741090051139066130)
XLA Ops:
  0.6 35.5 %shard_map.68.done_ref = f32[2,8,128]{2,1,0:T(8,128)} custom-call(s32[4096,128]{1,0:T(8,128)} %bins_ref.1, bf16[32,128]{1,0:T(8,128)(2,1)} %bitcast.6, bf16[32,128]{1,0:T(8,128)(2,1)} %bitcast.7, s32[32,128]{1,0:T(8,128)} %bitcast.5, s32[1,32]{1,0:T(1,128)} %bitcast.8), custom_call_target="tpu_custom_call" | custom-call | tf_op jit(solution)/shard_map/pallas_call | solution.py:464
  36.2 1.3 %shard_map.69 = (f32[8,16]{1,0:T(8,128)}, f32[16]{0:T(128)}) custom-call(f32[2,8,128]{2,1,0:T(8,128)} %shard_map.68.done_ref), custom_call_target="tpu_custom_call" | custom-call | tf_op jit(solution)/shard_map/pallas_call | solution.py:511

commit v4 on v3

--- a/solution.py
+++ b/solution.py
@@ -357,20 +357,28 @@
 
         return carry
 
-    lax.fori_loop(0, turns - 1, iteration, 0)
-
-    def closing(step, carry):
-        work(step, False)
-
-        pass_on(step)
-
-        @pl.when(step == turns - 2)
+    lax.fori_loop(0, turns - 2, iteration, 0)
+
+    def closing(slot, carry):
+        step = turns - 2 + lax.div(slot, 2)
+        is_p = lax.rem(slot, 2) == 0
+        work(step, is_p)
+
+        @pl.when(is_p)
+        def _():
+            pair_copy(group_of(step)[2]).start()
+
+        @pl.when(jnp.logical_not(is_p))
+        def _():
+            pass_on(step)
+
+        @pl.when(slot == 2)
         def _():
             do_f(relayed - 1)
 
         return carry
 
-    lax.fori_loop(turns - 2, turns, closing, 0)
+    lax.fori_loop(0, 4, closing, 0)
 
     hist = out[1, 2 * last, :, me_g]
     for k in range(relayed):

time: 37.7 us -> 37.4 us (level)
  no operation moved by 1% of the time
where the time goes in v4:
time: 37.4 us; the launch traced here: 37.2 us
  Pallas kernels  36.6 us (98%)
  between operations  0.64 us (2%)
    pallas_call x1, Pallas kernels, kernel_body(): pl.pallas_call(functools.partial(kernel, groups, devs, leaves), out_shape...  35.3 us
    pallas_call x1, Pallas kernels, kernel_body(): pl.pallas_call(finish, out_shape=(jax.ShapeDtypeStruct((per_dev, own_leav...  1.29 us

profile of v4, /device:TPU:0, one launch (start us, length us, event | category | flops | bytes accessed | tf_op | source)
XLA Modules:
  0.0 37.2 jit_solution(12856416706164403441)
XLA Ops:
  0.6 35.3 %shard_map.68.done_ref = f32[2,8,128]{2,1,0:T(8,128)} custom-call(s32[4096,128]{1,0:T(8,128)} %bins_ref.1, bf16[32,128]{1,0:T(8,128)(2,1)} %bitcast.6, bf16[32,128]{1,0:T(8,128)(2,1)} %bitcast.7, s32[32,128]{1,0:T(8,128)} %bitcast.5, s32[1,32]{1,0:T(1,128)} %bitcast.8), custom_call_target="tpu_custom_call" | custom-call | tf_op jit(solution)/shard_map/pallas_call | solution.py:472
  35.9 1.3 %shard_map.69 = (f32[8,16]{1,0:T(8,128)}, f32[16]{0:T(128)}) custom-call(f32[2,8,128]{2,1,0:T(8,128)} %shard_map.68.done_ref), custom_call_target="tpu_custom_call" | custom-call | tf_op jit(solution)/shard_map/pallas_call | solution.py:519

commit v5 on v4

--- a/solution.py
+++ b/solution.py
@@ -412,7 +412,6 @@
     gain_out[...] = tile
 
     gain_copy = remote(gain_out, gain_in, gain_sem, 0, y_dev)
-    gain_copy.start()
 
     def best_copy(step):
         return remote(gain_out.at[pl.ds(7, 1)], best_in.at[step], best_sem, step, nth(step))
@@ -420,6 +419,7 @@
     for step in range(1, everyone):
         if step != devs:
             best_copy(step).start()
+    gain_copy.start()
     for n in range(2 * planes):
         pair_copy(n).wait_send()
     for k in range(relayed):
@@ -428,7 +428,7 @@
     for k in range(relayed, planes):
         for number in direct(k):
             direct_copy(k, number).wait_send()
-    gain_copy.wait()
+    gain_copy.wait_recv()
     other = gain_in[...]
     top = jnp.maximum(top, other[7:8, :])
     low_tile = jnp.where(me_g == 0, tile, other)
@@ -437,10 +437,14 @@
     done_ref[0] = jnp.where(me_g == 0, gain, pltpu.roll(gain, LANES - own_leaves, 1))
     for step in range(1, everyone):
         if step != devs:
-            best_copy(step).wait()
+            best_copy(step).wait_recv()
             top = jnp.maximum(top, best_in[step])
     top = jnp.broadcast_to(top, (8, LANES))
     done_ref[1] = jnp.where(me_g == 0, top, pltpu.roll(top, LANES - own_leaves, 1))
+    gain_copy.wait_send()
+    for step in range(1, everyone):
+        if step != devs:
+            best_copy(step).wait_send()
 
 
 def finish(done_ref, gain_ref, best_ref):

time: 37.4 us -> 37.4 us (level)
  no operation moved by 1% of the time
where the time goes in v5:
time: 37.4 us; the launch traced here: 37.2 us
  Pallas kernels  36.6 us (98%)
  between operations  0.64 us (2%)
    pallas_call x1, Pallas kernels, kernel_body(): pl.pallas_call(functools.partial(kernel, groups, devs, leaves), out_shape...  35.3 us
    pallas_call x1, Pallas kernels, kernel_body(): pl.pallas_call(finish, out_shape=(jax.ShapeDtypeStruct((per_dev, own_leav...  1.29 us

profile of v5, /device:TPU:0, one launch (start us, length us, event | category | flops | bytes accessed | tf_op | source)
XLA Modules:
  0.0 37.2 jit_solution(14146860486905928858)
XLA Ops:
  0.6 35.3 %shard_map.68.done_ref = f32[2,8,128]{2,1,0:T(8,128)} custom-call(s32[4096,128]{1,0:T(8,128)} %bins_ref.1, bf16[32,128]{1,0:T(8,128)(2,1)} %bitcast.6, bf16[32,128]{1,0:T(8,128)(2,1)} %bitcast.7, s32[32,128]{1,0:T(8,128)} %bitcast.5, s32[1,32]{1,0:T(1,128)} %bitcast.8), custom_call_target="tpu_custom_call" | custom-call | tf_op jit(solution)/shard_map/pallas_call | solution.py:476
  35.9 1.3 %shard_map.69 = (f32[8,16]{1,0:T(8,128)}, f32[16]{0:T(128)}) custom-call(f32[2,8,128]{2,1,0:T(8,128)} %shard_map.68.done_ref), custom_call_target="tpu_custom_call" | custom-call | tf_op jit(solution)/shard_map/pallas_call | solution.py:523

commit v6 on v5

--- a/solution.py
+++ b/solution.py
@@ -10,7 +10,7 @@
 BINS = 64
 LANES = 128
 KCHUNK = 1024
-STEP_ROWS = 1024
+STEP_ROWS = 2048
 
 
 reg_lambda = 1.0
@@ -536,7 +536,7 @@
     planes = devs // 4
     if groups != 2 or devs % 4 or planes != 4 or leaves != 32:
         return False
-    return features == 8 * devs and rows % KCHUNK == 0
+    return features == 8 * devs and rows % KCHUNK == 0 and rows % STEP_ROWS == 0
 
 
 def solution(mesh):

time: 37.4 us -> 37.5 us (level)
  no operation moved by 1% of the time
where the time goes in v6:
time: 37.5 us; the launch traced here: 37.2 us
  Pallas kernels  36.6 us (98%)
  between operations  0.64 us (2%)
    pallas_call x1, Pallas kernels, kernel_body(): pl.pallas_call(functools.partial(kernel, groups, devs, leaves), out_shape...  35.3 us
    pallas_call x1, Pallas kernels, kernel_body(): pl.pallas_call(finish, out_shape=(jax.ShapeDtypeStruct((per_dev, own_leav...  1.29 us

profile of v6, /device:TPU:0, one launch (start us, length us, event | category | flops | bytes accessed | tf_op | source)
XLA Modules:
  0.0 37.2 jit_solution(12600151279167253613)
XLA Ops:
  0.6 35.3 %shard_map.68.done_ref = f32[2,8,128]{2,1,0:T(8,128)} custom-call(s32[4096,128]{1,0:T(8,128)} %bins_ref.1, bf16[32,128]{1,0:T(8,128)(2,1)} %bitcast.6, bf16[32,128]{1,0:T(8,128)(2,1)} %bitcast.7, s32[32,128]{1,0:T(8,128)} %bitcast.5, s32[1,32]{1,0:T(1,128)} %bitcast.8), custom_call_target="tpu_custom_call" | custom-call | tf_op jit(solution)/shard_map/pallas_call | solution.py:476
  35.9 1.3 %shard_map.69 = (f32[8,16]{1,0:T(8,128)}, f32[16]{0:T(128)}) custom-call(f32[2,8,128]{2,1,0:T(8,128)} %shard_map.68.done_ref), custom_call_target="tpu_custom_call" | custom-call | tf_op jit(solution)/shard_map/pallas_call | solution.py:523
